TPU v7x, 32 devices: a whole 2x2x4 slice. The times are simulated.
32 devices in a mesh: blk: 16 (over z, y, core), head: 2 (over x).
Axes of the slice: x: 2, y: 2, z: 4, core: 2. Of those that a mesh axis runs over, the one named last changes fastest.
Arguments:
- queries: bfloat16 [4096, 1024], P('blk', 'head'), may hold values from -216 to 216
- keys: bfloat16 [4096, 1024], P('blk', 'head'), may hold values from -6 to 6
- values: bfloat16 [4096, 1024], P('blk', 'head'), may hold values from -6 to 6
- group_table: int32 [16, 2], P('blk'), may hold values from 0 to 31, as said below
- doc_ids: int32 [4096], replicated, may hold values from 0 to 15, never falling along the last dimension, each value on 1 to 2048 neighbouring positions
Outputs:
- attended: bfloat16 [4096, 1024], P('blk', 'head')
Inputs may be any that keep to these rules, and one draw needn't show every extreme that they name: group_table[d, 1] = 31 - group_table[d, 0]; the first column holds each of 0 to 15 once. `doc_ids`: document numbers never fall along positions; a document holds at most 2048 positions.
All inputs are finite; a program needn't handle non-finite values.
Results may differ from a plain program's by a relative error of at most 0.0049.
Values may be sent and summed in bfloat16 or wider, within the bound.
A program may use at most 192 MiB of HBM per device.

v0:
```python
import math
import jax
import jax.numpy as jnp
from jax import lax
from jax.sharding import PartitionSpec as P

HEAD_DIM = 128


def shards(queries, keys, values, group_table, doc_ids):
    tok_rows = queries.shape[0]
    group_rows = tok_rows // 2
    head_count = queries.shape[1] // HEAD_DIM
    score_scale = 1.0 / math.sqrt(HEAD_DIM)
    whole_table = lax.all_gather(group_table, "blk", axis=0, tiled=True)
    group_docs = doc_ids.reshape(doc_ids.shape[0] // group_rows, group_rows)
    within = jnp.arange(group_rows, dtype=jnp.int32)
    stored_groups = whole_table.reshape(-1)
    all_key_pos = (stored_groups[:, None] * group_rows + within[None, :]).reshape(-1)
    all_key_doc = group_docs[stored_groups].reshape(-1)
    local_groups = group_table.reshape(-1)
    query_pos = (local_groups[:, None] * group_rows + within[None, :]).reshape(-1)
    query_doc = group_docs[local_groups].reshape(-1)
    query_heads = queries.reshape(tok_rows, head_count, HEAD_DIM)

    def attend_shard(running_state, key_piece, value_piece, offset):
        piece_rows = key_piece.shape[0]
        key_pos = lax.dynamic_slice_in_dim(all_key_pos, offset, piece_rows, 0)
        key_doc = lax.dynamic_slice_in_dim(all_key_doc, offset, piece_rows, 0)
        visible = (query_doc[:, None] == key_doc[None, :]) & (
            key_pos[None, :] <= query_pos[:, None]
        )
        summed, running_max, weight_sum = running_state
        key_heads = key_piece.reshape(piece_rows, head_count, HEAD_DIM)
        value_heads = value_piece.reshape(piece_rows, head_count, HEAD_DIM)
        scores = (
            jnp.einsum("qhd,khd->hqk", query_heads, key_heads, preferred_element_type=jnp.float32)
            * score_scale
        )
        scores = jnp.where(visible[None], scores, -1e30)
        new_max = jnp.maximum(running_max, jnp.max(scores, axis=-1))
        weights = jnp.where(visible[None], jnp.exp(scores - new_max[..., None]), 0.0)
        factor = jnp.exp(running_max - new_max)
        weight_sum = weight_sum * factor + jnp.sum(weights, axis=-1)
        summed = summed * jnp.transpose(factor)[..., None] + jnp.einsum(
            "hqk,khd->qhd",
            weights.astype(jnp.bfloat16),
            value_heads,
            preferred_element_type=jnp.float32,
        )
        return (summed, new_max, weight_sum)

    initial = (
        jnp.zeros((tok_rows, head_count, HEAD_DIM), jnp.float32),
        jnp.full((head_count, tok_rows), -1e30, jnp.float32),
        jnp.zeros((head_count, tok_rows), jnp.float32),
    )
    key_piece = lax.all_gather(keys, "blk", axis=0, tiled=True)
    value_piece = lax.all_gather(values, "blk", axis=0, tiled=True)
    shard_count = key_piece.shape[0] // tok_rows
    key_shards = key_piece.reshape(shard_count, tok_rows, key_piece.shape[1])
    value_shards = value_piece.reshape(shard_count, tok_rows, value_piece.shape[1])
    shard_ids = jnp.arange(shard_count, dtype=jnp.int32)

    def step(state_now, item):
        key_one, value_one, shard_index = item
        start = shard_index * tok_rows
        return (attend_shard(state_now, key_one, value_one, start), None)

    final_state, unused = lax.scan(step, initial, (key_shards, value_shards, shard_ids))
    summed, running_max, weight_sum = final_state
    output = summed / jnp.transpose(weight_sum)[..., None]
    return output.reshape(tok_rows, head_count * HEAD_DIM).astype(jnp.bfloat16)


def solution(mesh):
    in_specs = (P("blk", "head"), P("blk", "head"), P("blk", "head"), P("blk", None), P())
    out_specs = P("blk", "head")
    return jax.shard_map(shards, mesh=mesh, in_specs=in_specs, out_specs=out_specs, check_vma=False)
```

profile of v0, /device:TPU:0, one launch (start us, length us, event | category | flops | bytes accessed | tf_op | source)
XLA Modules:
  0.0 186.2 jit_solution(14628548293793121357)
XLA Ops:
  6.5 0.7 all-gather.4.cloned.1.call-update
  7.3 0.7 all-gather.6.cloned.1.call-update
  8.0 23.3 %all-gather = s32[16,1,2]{2,1,0:T(1,128)S(1)} all-gather(s32[1,1,2]{2,1,0:T(1,128)} %bitcast.68), channel_id=1, replica_groups=mesh['blk'=16,'head'=2] {'blk'}, dimensions={0}, use_global_device_ids=true | all-gather | bytes 136 | tf_op jit(solution)/shard_map/all_gather | solution.py:15
  31.4 0.5 broadcast.150
  31.9 0.7 multiply_reduce_fusion
  32.8 0.6 gather_fusion.1
  33.3 0.7 fusion.14
  34.0 0.6 gather_fusion
  34.6 1.1 copy.23
  35.8 0.7 multiply_bitcast_fusion
  36.6 26.1 %all-gather.4.cloned.1.call-done = bf16[4096,512]{1,0:T(8,128)(2,1)} async-done(((bf16[256,512]{1,0:T(8,128)(2,1)}), bf16[4096,512]{1,0:T(8,128)(2,1)}) %all-gather.4.cloned.1.call-update) | async-done | bytes 4194320 | tf_op jit(solution)/shard_map/all_gather | solution.py:58
  62.7 51.1 %all-gather.6.cloned.1.call-done = bf16[4096,512]{1,0:T(8,128)(2,1)} async-done(((bf16[256,512]{1,0:T(8,128)(2,1)}), bf16[4096,512]{1,0:T(8,128)(2,1)}) %all-gather.6.cloned.1.call-update) | async-done | bytes 4194320 | tf_op jit(solution)/shard_map/all_gather | solution.py:59
  113.8 64.7 %while.15 = (s32[]{:T(128)}, f32[256,4,128]{0,2,1:T(8,128)S(1)}, f32[4,256]{1,0:T(4,128)S(1)}, f32[4,256]{1,0:T(4,128)S(1)}, s32[2,128]{1,0:T(2,128)S(1)}, /*ind...) while((s32[]{:T(128)}, f32[256,4,128]{0,2,1:T(8,128)S(1)}, ...), condition=%wide.region_3.4_spmd.clone, body=%wide.region_0.3_spmd.clone.sunk | while | flops 137173248 | bytes 7415023 | solution.py:70
  113.8 0.6 dynamic_slice.29
  115.4 1.1 constant_dynamic-slice_fusion.3
  116.6 0.4 fusion.33
  117.4 0.4 fusion.35
  117.8 0.6 dynamic_slice.29
  119.4 1.1 constant_dynamic-slice_fusion.3
  120.6 0.4 fusion.33
  121.4 0.4 fusion.35
  121.9 0.6 dynamic_slice.29
  123.5 1.1 constant_dynamic-slice_fusion.3
  125.4 0.4 fusion.35
  125.9 0.6 dynamic_slice.29
  127.5 1.1 constant_dynamic-slice_fusion.3
  129.5 0.4 fusion.35
  129.9 0.6 dynamic_slice.29
  131.5 1.1 constant_dynamic-slice_fusion.3
  133.5 0.4 fusion.35
  134.0 0.6 dynamic_slice.29
  135.6 1.1 constant_dynamic-slice_fusion.3
  137.6 0.4 fusion.35
  138.0 0.6 dynamic_slice.29
  139.6 1.1 constant_dynamic-slice_fusion.3
  141.6 0.4 fusion.35
  142.1 0.6 dynamic_slice.29
  143.7 1.1 constant_dynamic-slice_fusion.3
  145.7 0.4 fusion.35
  146.1 0.6 dynamic_slice.29
  147.7 1.1 constant_dynamic-slice_fusion.3
  149.7 0.4 fusion.35
  150.2 0.6 dynamic_slice.29
  151.8 1.1 constant_dynamic-slice_fusion.3
  153.7 0.4 fusion.35
  154.2 0.6 dynamic_slice.29
  155.8 1.1 constant_dynamic-slice_fusion.3
  157.8 0.4 fusion.35
  158.2 0.6 dynamic_slice.29
  159.8 1.1 constant_dynamic-slice_fusion.3
  161.8 0.4 fusion.35
  162.3 0.6 dynamic_slice.29
  163.9 1.1 constant_dynamic-slice_fusion.3
  165.9 0.4 fusion.35
  166.3 0.6 dynamic_slice.29
  167.9 1.1 constant_dynamic-slice_fusion.3
  169.9 0.4 fusion.35
  170.4 0.6 dynamic_slice.29
  172.0 1.1 constant_dynamic-slice_fusion.3
  174.0 0.4 fusion.35
  174.4 0.6 dynamic_slice.29
  176.0 1.1 constant_dynamic-slice_fusion.3
  178.0 0.4 fusion.35
  178.5 0.8 copy.30
  (190 shorter events, 19.6 us)
Async XLA Ops:
  6.5 26.2 %copy-start = (s32[4096]{0:T(1024)S(1)}, s32[4096]{0:T(1024)}, u32[]{:S(2)}) copy-start(s32[4096]{0:T(1024)} %param.11) | copy-start | bytes 49156
  6.5 56.1 %all-gather.4.cloned.1.call-start = ((), (), s32[]{:S(2)}) async-start(), calls=%async_computation | async-start | bytes 4456448 | tf_op jit(solution)/shard_map/all_gather | solution.py:58
  7.3 106.5 %all-gather.6.cloned.1.call-start = ((), (), s32[]{:S(2)}) async-start(), calls=%async_computation.1 | async-start | bytes 4456448 | tf_op jit(solution)/shard_map/all_gather | solution.py:59
Sparse Core Ops, SparseCore 0:
  9.5 53.1 all-gather.3
  64.8 48.8 all-gather.5
where the time goes:
time: 187 us; the launch traced here: 186 us
  waiting for transfers between devices  78.6 us (42%)
  local copies, waits for them, and re-layouts  37.4 us (20%)
  blocking collectives  23.3 us (12%)
  between operations  13.5 us (7%)
  matrix products  12.7 us (7%)
  loops' own time  11.4 us (6%)
  other arithmetic  9.23 us (5%)
    all_gather x1, waiting for transfers between devices, shards(): value_piece = lax.all_gather(values, 'blk', axis=0, tiled=True)  51.1 us
    dynamic_slice x64, local copies, waits for them, and re-layouts, shards(): lax.scan(step, initial, (key_shards, value_shards, shard_ids))  31 us
    all_gather x1, waiting for transfers between devices, shards(): key_piece = lax.all_gather(keys, 'blk', axis=0, tiled=True)  26.1 us
    all_gather x1, blocking collectives, shards(): whole_table = lax.all_gather(group_table, 'blk', axis=0, tiled=True)  23.3 us
    another operation x1, loops' own time, shards(): lax.scan(step, initial, (key_shards, value_shards, shard_ids))  11.4 us
    dot_general x16, matrix products, attend_shard(): jnp.einsum('hqk,khd->qhd', weights.astype(jnp.bfloat16), value_heads, pre...  6.68 us
    dot_general x16, matrix products, attend_shard(): jnp.einsum('qhd,khd->hqk', query_heads, key_heads, preferred_element_type...  6.02 us
  transfers between devices with their start and end apart: 2, of which 2 were waited for; matrix products, arithmetic and copies ran while one was open for 3% of the time, Pallas kernels for 0%

commit v1 on v0

--- a/solution.py
+++ b/solution.py
@@ -56,7 +56,12 @@
         jnp.zeros((head_count, tok_rows), jnp.float32),
     )
     key_piece = lax.all_gather(keys, "blk", axis=0, tiled=True)
-    value_piece = lax.all_gather(values, "blk", axis=0, tiled=True)
+    ring = [values]
+    for hop in range(15):
+        ring.append(lax.ppermute(ring[-1], "blk", [(dev, (dev + 1) % 16) for dev in range(16)]))
+    value_piece = jnp.roll(
+        jnp.concatenate(ring[::-1], axis=0), (lax.axis_index("blk") + 1) * ring[0].shape[0], axis=0
+    )
     shard_count = key_piece.shape[0] // tok_rows
     key_shards = key_piece.reshape(shard_count, tok_rows, key_piece.shape[1])
     value_shards = value_piece.reshape(shard_count, tok_rows, value_piece.shape[1])

time: 187 us -> 245 us (1.31)
  waiting for transfers between devices: 78.6 us -> 126 us
  local copies, waits for them, and re-layouts: 37.4 us -> 50.3 us
  blocking collectives: 23.3 us -> 18.2 us
    ppermute x0 -> x15, waiting for transfers between devices: none -> 126 us  [shards(): lax.ppermute(ring[-1], 'blk', [(dev, (dev + 1) % 16) for dev in range(16)])]
    all_gather x1 -> x0, waiting for transfers between devices: 51.1 us -> none  [shards(): value_piece = lax.all_gather(values, 'blk', axis=0, tiled=True)]
    all_gather x1, waiting for transfers between devices: 26.1 us -> 0.01 us  [shards(): key_piece = lax.all_gather(keys, 'blk', axis=0, tiled=True)]
    unnamed x4 -> x49, local copies, waits for them, and re-layouts: 1.26 us -> 12.1 us
    all_gather x1, blocking collectives: 23.3 us -> 18.2 us  [shards(): whole_table = lax.all_gather(group_table, 'blk', axis=0, tiled=True)]
  transfers between devices with their start and end apart: 2 -> 16, of which waited for: 2 -> 14; matrix products, arithmetic and copies ran while one was open for 3% -> 8% of each run, Pallas kernels for 0% -> 0%
where the time goes in v1:
time: 245 us; the launch traced here: 243 us
  waiting for transfers between devices  126 us (51%)
  local copies, waits for them, and re-layouts  50.3 us (21%)
  blocking collectives  18.2 us (7%)
  between operations  13.8 us (6%)
  matrix products  12.5 us (5%)
  loops' own time  11.7 us (5%)
  other arithmetic  9.24 us (4%)
    ppermute x15, waiting for transfers between devices, shards(): lax.ppermute(ring[-1], 'blk', [(dev, (dev + 1) % 16) for dev in range(16)])  126 us
    dynamic_slice x64, local copies, waits for them, and re-layouts, shards(): lax.scan(step, initial, (key_shards, value_shards, shard_ids))  30.8 us
    all_gather x1, blocking collectives, shards(): whole_table = lax.all_gather(group_table, 'blk', axis=0, tiled=True)  18.2 us
    unnamed x49, local copies, waits for them, and re-layouts  12.1 us
    another operation x1, loops' own time, shards(): lax.scan(step, initial, (key_shards, value_shards, shard_ids))  11.7 us
    dot_general x16, matrix products, attend_shard(): jnp.einsum('hqk,khd->qhd', weights.astype(jnp.bfloat16), value_heads, pre...  6.56 us
    dot_general x16, matrix products, attend_shard(): jnp.einsum('qhd,khd->hqk', query_heads, key_heads, preferred_element_type...  5.93 us
  transfers between devices with their start and end apart: 16, of which 14 were waited for; matrix products, arithmetic and copies ran while one was open for 8% of the time, Pallas kernels for 0%

profile of v1, /device:TPU:0, one launch (start us, length us, event | category | flops | bytes accessed | tf_op | source)
XLA Modules:
  0.0 242.5 jit_solution(11480840652181795494)
XLA Ops:
  7.0 9.3 %collective-permute-done = bf16[256,512]{1,0:T(8,128)(2,1)S(1)} collective-permute-done((bf16[256,512]{1,0:T(8,128)(2,1)}, bf16[256,512]{1,0:T(8,128)(2,1)S(1)}, u32[]{:S(2)}, u32[]{:S(2)}) %collective-permute-start) | collective-permute-done | bytes 262176 | tf_op jit(solution)/shard_map/ppermute | solution.py:61
  16.3 8.5 %collective-permute-done.1 = bf16[256,512]{1,0:T(8,128)(2,1)S(1)} collective-permute-done((bf16[256,512]{1,0:T(8,128)(2,1)S(1)}, bf16[256,512]{1,0:T(8,128)(2,1)S(1)}, u32[]{:S(2)}, u32[]{:S(2)}) %collective-permute-start.1) | collective-permute-done | bytes 262176 | tf_op jit(solution)/shard_map/ppermute | solution.py:61
  24.8 8.5 %collective-permute-done.2 = bf16[256,512]{1,0:T(8,128)(2,1)S(1)} collective-permute-done((bf16[256,512]{1,0:T(8,128)(2,1)S(1)}, bf16[256,512]{1,0:T(8,128)(2,1)S(1)}, u32[]{:S(2)}, u32[]{:S(2)}) %collective-permute-start.2) | collective-permute-done | bytes 262176 | tf_op jit(solution)/shard_map/ppermute | solution.py:61
  33.3 11.7 %collective-permute-done.3 = bf16[256,512]{1,0:T(8,128)(2,1)S(1)} collective-permute-done((bf16[256,512]{1,0:T(8,128)(2,1)S(1)}, bf16[256,512]{1,0:T(8,128)(2,1)S(1)}, u32[]{:S(2)}, u32[]{:S(2)}) %collective-permute-start.3) | collective-permute-done | bytes 262176 | tf_op jit(solution)/shard_map/ppermute | solution.py:61
  45.0 8.7 %collective-permute-done.4 = bf16[256,512]{1,0:T(8,128)(2,1)S(1)} collective-permute-done((bf16[256,512]{1,0:T(8,128)(2,1)S(1)}, bf16[256,512]{1,0:T(8,128)(2,1)S(1)}, u32[]{:S(2)}, u32[]{:S(2)}) %collective-permute-start.4) | collective-permute-done | bytes 262176 | tf_op jit(solution)/shard_map/ppermute | solution.py:61
  53.7 11.9 %collective-permute-done.5 = bf16[256,512]{1,0:T(8,128)(2,1)S(1)} collective-permute-done((bf16[256,512]{1,0:T(8,128)(2,1)S(1)}, bf16[256,512]{1,0:T(8,128)(2,1)S(1)}, u32[]{:S(2)}, u32[]{:S(2)}) %collective-permute-start.5) | collective-permute-done | bytes 262176 | tf_op jit(solution)/shard_map/ppermute | solution.py:61
  65.6 13.8 %collective-permute-done.6 = bf16[256,512]{1,0:T(8,128)(2,1)S(1)} collective-permute-done((bf16[256,512]{1,0:T(8,128)(2,1)S(1)}, bf16[256,512]{1,0:T(8,128)(2,1)S(1)}, u32[]{:S(2)}, u32[]{:S(2)}) %collective-permute-start.6) | collective-permute-done | bytes 262176 | tf_op jit(solution)/shard_map/ppermute | solution.py:61
  79.5 8.5 %collective-permute-done.7 = bf16[256,512]{1,0:T(8,128)(2,1)S(1)} collective-permute-done((bf16[256,512]{1,0:T(8,128)(2,1)S(1)}, bf16[256,512]{1,0:T(8,128)(2,1)S(1)}, u32[]{:S(2)}, u32[]{:S(2)}) %collective-permute-start.7) | collective-permute-done | bytes 262176 | tf_op jit(solution)/shard_map/ppermute | solution.py:61
  88.0 8.5 %collective-permute-done.8 = bf16[256,512]{1,0:T(8,128)(2,1)S(1)} collective-permute-done((bf16[256,512]{1,0:T(8,128)(2,1)S(1)}, bf16[256,512]{1,0:T(8,128)(2,1)S(1)}, u32[]{:S(2)}, u32[]{:S(2)}) %collective-permute-start.8) | collective-permute-done | bytes 262176 | tf_op jit(solution)/shard_map/ppermute | solution.py:61
  96.4 8.5 %collective-permute-done.9 = bf16[256,512]{1,0:T(8,128)(2,1)S(1)} collective-permute-done((bf16[256,512]{1,0:T(8,128)(2,1)S(1)}, bf16[256,512]{1,0:T(8,128)(2,1)S(1)}, u32[]{:S(2)}, u32[]{:S(2)}) %collective-permute-start.9) | collective-permute-done | bytes 262176 | tf_op jit(solution)/shard_map/ppermute | solution.py:61
  104.9 8.5 %collective-permute-done.10 = bf16[256,512]{1,0:T(8,128)(2,1)S(1)} collective-permute-done((bf16[256,512]{1,0:T(8,128)(2,1)S(1)}, bf16[256,512]{1,0:T(8,128)(2,1)S(1)}, u32[]{:S(2)}, u32[]{:S(2)}) %collective-permute-start.10) | collective-permute-done | bytes 262176 | tf_op jit(solution)/shard_map/ppermute | solution.py:61
  113.4 18.2 %all-gather = s32[16,1,2]{2,1,0:T(1,128)S(1)} all-gather(s32[1,1,2]{2,1,0:T(1,128)} %bitcast.68), channel_id=1, replica_groups=mesh['blk'=16,'head'=2] {'blk'}, dimensions={0}, use_global_device_ids=true | all-gather | bytes 136 | tf_op jit(solution)/shard_map/all_gather | solution.py:15
  131.6 0.7 fusion.14
  132.9 0.7 multiply_reduce_fusion
  133.7 7.1 %collective-permute-done.12 = bf16[256,512]{1,0:T(8,128)(2,1)} collective-permute-done((bf16[256,512]{1,0:T(8,128)(2,1)S(1)}, bf16[256,512]{1,0:T(8,128)(2,1)}, u32[]{:S(2)}, u32[]{:S(2)}) %collective-permute-start.12) | collective-permute-done | bytes 262176 | tf_op jit(solution)/shard_map/ppermute | solution.py:61
  140.9 0.7 multiply_bitcast_fusion
  141.5 8.1 %collective-permute-done.13 = bf16[256,512]{1,0:T(8,128)(2,1)} collective-permute-done((bf16[256,512]{1,0:T(8,128)(2,1)}, bf16[256,512]{1,0:T(8,128)(2,1)}, u32[]{:S(2)}, u32[]{:S(2)}) %collective-permute-start.13) | collective-permute-done | bytes 262176 | tf_op jit(solution)/shard_map/ppermute | solution.py:61
  151.0 1.8 copy.23
  152.8 1.1 copy.25
  154.0 4.5 %collective-permute-done.14 = bf16[256,512]{1,0:T(8,128)(2,1)} collective-permute-done((bf16[256,512]{1,0:T(8,128)(2,1)}, bf16[256,512]{1,0:T(8,128)(2,1)}, u32[]{:S(2)}, u32[]{:S(2)}) %collective-permute-start.14) | collective-permute-done | bytes 262176 | tf_op jit(solution)/shard_map/ppermute | solution.py:61
  158.5 1.0 constant_dynamic-update-slice_fusion.31
  159.5 1.0 constant_dynamic-update-slice_fusion.30
  160.4 1.0 constant_dynamic-update-slice_fusion.29
  161.4 1.0 constant_dynamic-update-slice_fusion.28
  162.4 1.0 constant_dynamic-update-slice_fusion.27
  163.3 1.0 constant_dynamic-update-slice_fusion.26
  164.6 1.0 constant_dynamic-update-slice_fusion.15
  165.6 1.0 constant_dynamic-update-slice_fusion.14
  166.5 1.0 constant_dynamic-update-slice_fusion.13
  167.9 2.3 constant_dynamic-slice_fusion.2
  170.2 64.6 %while.15 = (s32[]{:T(128)}, f32[256,4,128]{0,2,1:T(8,128)S(1)}, f32[4,256]{1,0:T(4,128)S(1)}, f32[4,256]{1,0:T(4,128)S(1)}, s32[2,128]{1,0:T(2,128)S(1)}, /*ind...) while((s32[]{:T(128)}, f32[256,4,128]{0,2,1:T(8,128)S(1)}, ...), condition=%wide.region_3.4_spmd.clone, body=%wide.region_0.3_spmd.clone.sunk | while | flops 137173248 | bytes 7415023 | solution.py:75
  170.2 0.6 dynamic_slice.35
  171.8 1.1 constant_dynamic-slice_fusion.4
  174.2 0.6 dynamic_slice.35
  175.8 1.1 constant_dynamic-slice_fusion.4
  178.3 0.6 dynamic_slice.35
  179.9 1.1 constant_dynamic-slice_fusion.4
  182.3 0.6 dynamic_slice.35
  183.9 1.1 constant_dynamic-slice_fusion.4
  186.3 0.6 dynamic_slice.35
  187.9 1.1 constant_dynamic-slice_fusion.4
  190.4 0.6 dynamic_slice.35
  192.0 1.1 constant_dynamic-slice_fusion.4
  194.4 0.6 dynamic_slice.35
  196.0 1.1 constant_dynamic-slice_fusion.4
  198.4 0.6 dynamic_slice.35
  200.1 1.1 constant_dynamic-slice_fusion.4
  202.5 0.6 dynamic_slice.35
  204.1 1.1 constant_dynamic-slice_fusion.4
  206.5 0.6 dynamic_slice.35
  208.1 1.1 constant_dynamic-slice_fusion.4
  210.6 0.6 dynamic_slice.35
  212.2 1.1 constant_dynamic-slice_fusion.4
  214.6 0.6 dynamic_slice.35
  216.2 1.1 constant_dynamic-slice_fusion.4
  218.6 0.6 dynamic_slice.35
  220.2 1.1 constant_dynamic-slice_fusion.4
  222.7 0.6 dynamic_slice.35
  224.3 1.1 constant_dynamic-slice_fusion.4
  226.7 0.6 dynamic_slice.35
  228.3 1.1 constant_dynamic-slice_fusion.4
  230.7 0.6 dynamic_slice.35
  232.4 1.1 constant_dynamic-slice_fusion.4
  234.8 0.8 copy.30
  (264 shorter events, 29.5 us)
Async XLA Ops:
  6.5 143.3 %copy-start = (s32[4096]{0:T(1024)S(1)}, s32[4096]{0:T(1024)}, u32[]{:S(2)}) copy-start(s32[4096]{0:T(1024)} %param.11) | copy-start | bytes 49156
  6.5 158.0 %copy-start.1 = (bf16[256,512]{1,0:T(8,128)(2,1)S(1)}, bf16[256,512]{1,0:T(8,128)(2,1)}, u32[]{:S(2)}) copy-start(bf16[256,512]{1,0:T(8,128)(2,1)} %param.9) | copy-start | bytes 786436
  6.5 163.6 %all-gather.3.cloned.1.call-start = ((), (), s32[]{:S(2)}) async-start(), calls=%async_computation | async-start | bytes 4456448 | tf_op jit(solution)/shard_map/all_gather | solution.py:58
  6.5 9.8 %collective-permute-start = (bf16[256,512]{1,0:T(8,128)(2,1)}, bf16[256,512]{1,0:T(8,128)(2,1)S(1)}, u32[]{:S(2)}, u32[]{:S(2)}) collective-permute-start(bf16[256,512]{1,0:T(8,128)(2,1)} %param.9), channel_id=1, source_target_pairs={{0,2},{2,4},{4,6},{6,8},{8,10},{10,12},{12,14},{14,16},{16,18},{18... | collective-permute-start | bytes 786440 | tf_op jit(solution)/shard_map/ppermute | solution.py:61
  16.3 8.5 %collective-permute-start.1 = (bf16[256,512]{1,0:T(8,128)(2,1)S(1)}, bf16[256,512]{1,0:T(8,128)(2,1)S(1)}, u32[]{:S(2)}, u32[]{:S(2)}) collective-permute-start(bf16[256,512]{1,0:T(8,128)(2,1)S(1)} %collective-permute-done), channel_id=1, source_target_pairs={{0,2},{2,4},{4,6},{6,8},{8,10},{10,12},{12,14},{14,16},{16,18},{18... | collective-permute-start | bytes 786440 | tf_op jit(solution)/shard_map/ppermute | solution.py:61
  24.8 8.5 %collective-permute-start.2 = (bf16[256,512]{1,0:T(8,128)(2,1)S(1)}, bf16[256,512]{1,0:T(8,128)(2,1)S(1)}, u32[]{:S(2)}, u32[]{:S(2)}) collective-permute-start(bf16[256,512]{1,0:T(8,128)(2,1)S(1)} %collective-permute-done.1), channel_id=1, source_target_pairs={{0,2},{2,4},{4,6},{6,8},{8,10},{10,12},{12,14},{14,16},{16,18},{18... | collective-permute-start | bytes 786440 | tf_op jit(solution)/shard_map/ppermute | solution.py:61
  33.3 11.7 %collective-permute-start.3 = (bf16[256,512]{1,0:T(8,128)(2,1)S(1)}, bf16[256,512]{1,0:T(8,128)(2,1)S(1)}, u32[]{:S(2)}, u32[]{:S(2)}) collective-permute-start(bf16[256,512]{1,0:T(8,128)(2,1)S(1)} %collective-permute-done.2), channel_id=1, source_target_pairs={{0,2},{2,4},{4,6},{6,8},{8,10},{10,12},{12,14},{14,16},{16,18},{18... | collective-permute-start | bytes 786440 | tf_op jit(solution)/shard_map/ppermute | solution.py:61
  45.0 8.7 %collective-permute-start.4 = (bf16[256,512]{1,0:T(8,128)(2,1)S(1)}, bf16[256,512]{1,0:T(8,128)(2,1)S(1)}, u32[]{:S(2)}, u32[]{:S(2)}) collective-permute-start(bf16[256,512]{1,0:T(8,128)(2,1)S(1)} %collective-permute-done.3), channel_id=1, source_target_pairs={{0,2},{2,4},{4,6},{6,8},{8,10},{10,12},{12,14},{14,16},{16,18},{18... | collective-permute-start | bytes 786440 | tf_op jit(solution)/shard_map/ppermute | solution.py:61
  53.7 11.9 %collective-permute-start.5 = (bf16[256,512]{1,0:T(8,128)(2,1)S(1)}, bf16[256,512]{1,0:T(8,128)(2,1)S(1)}, u32[]{:S(2)}, u32[]{:S(2)}) collective-permute-start(bf16[256,512]{1,0:T(8,128)(2,1)S(1)} %collective-permute-done.4), channel_id=1, source_target_pairs={{0,2},{2,4},{4,6},{6,8},{8,10},{10,12},{12,14},{14,16},{16,18},{18... | collective-permute-start | bytes 786440 | tf_op jit(solution)/shard_map/ppermute | solution.py:61
  65.6 13.8 %collective-permute-start.6 = (bf16[256,512]{1,0:T(8,128)(2,1)S(1)}, bf16[256,512]{1,0:T(8,128)(2,1)S(1)}, u32[]{:S(2)}, u32[]{:S(2)}) collective-permute-start(bf16[256,512]{1,0:T(8,128)(2,1)S(1)} %collective-permute-done.5), channel_id=1, source_target_pairs={{0,2},{2,4},{4,6},{6,8},{8,10},{10,12},{12,14},{14,16},{16,18},{18... | collective-permute-start | bytes 786440 | tf_op jit(solution)/shard_map/ppermute | solution.py:61
  79.5 8.5 %collective-permute-start.7 = (bf16[256,512]{1,0:T(8,128)(2,1)S(1)}, bf16[256,512]{1,0:T(8,128)(2,1)S(1)}, u32[]{:S(2)}, u32[]{:S(2)}) collective-permute-start(bf16[256,512]{1,0:T(8,128)(2,1)S(1)} %collective-permute-done.6), channel_id=1, source_target_pairs={{0,2},{2,4},{4,6},{6,8},{8,10},{10,12},{12,14},{14,16},{16,18},{18... | collective-permute-start | bytes 786440 | tf_op jit(solution)/shard_map/ppermute | solution.py:61
  87.9 8.5 %collective-permute-start.8 = (bf16[256,512]{1,0:T(8,128)(2,1)S(1)}, bf16[256,512]{1,0:T(8,128)(2,1)S(1)}, u32[]{:S(2)}, u32[]{:S(2)}) collective-permute-start(bf16[256,512]{1,0:T(8,128)(2,1)S(1)} %collective-permute-done.7), channel_id=1, source_target_pairs={{0,2},{2,4},{4,6},{6,8},{8,10},{10,12},{12,14},{14,16},{16,18},{18... | collective-permute-start | bytes 786440 | tf_op jit(solution)/shard_map/ppermute | solution.py:61
  96.4 8.5 %collective-permute-start.9 = (bf16[256,512]{1,0:T(8,128)(2,1)S(1)}, bf16[256,512]{1,0:T(8,128)(2,1)S(1)}, u32[]{:S(2)}, u32[]{:S(2)}) collective-permute-start(bf16[256,512]{1,0:T(8,128)(2,1)S(1)} %collective-permute-done.8), channel_id=1, source_target_pairs={{0,2},{2,4},{4,6},{6,8},{8,10},{10,12},{12,14},{14,16},{16,18},{18... | collective-permute-start | bytes 786440 | tf_op jit(solution)/shard_map/ppermute | solution.py:61
  104.9 44.8 %copy-start.2 = (bf16[256,512]{1,0:T(8,128)(2,1)}, bf16[256,512]{1,0:T(8,128)(2,1)S(1)}, u32[]{:S(2)}) copy-start(bf16[256,512]{1,0:T(8,128)(2,1)S(1)} %collective-permute-done.9) | copy-start | bytes 786436
  104.9 8.5 %collective-permute-start.10 = (bf16[256,512]{1,0:T(8,128)(2,1)S(1)}, bf16[256,512]{1,0:T(8,128)(2,1)S(1)}, u32[]{:S(2)}, u32[]{:S(2)}) collective-permute-start(bf16[256,512]{1,0:T(8,128)(2,1)S(1)} %collective-permute-done.9), channel_id=1, source_target_pairs={{0,2},{2,4},{4,6},{6,8},{8,10},{10,12},{12,14},{14,16},{16,18},{18... | collective-permute-start | bytes 786440 | tf_op jit(solution)/shard_map/ppermute | solution.py:61
  113.4 36.3 %copy-start.4 = (bf16[256,512]{1,0:T(8,128)(2,1)}, bf16[256,512]{1,0:T(8,128)(2,1)S(1)}, u32[]{:S(2)}) copy-start(bf16[256,512]{1,0:T(8,128)(2,1)S(1)} %collective-permute-done.10) | copy-start | bytes 786436
  113.4 18.8 %collective-permute-start.11 = (bf16[256,512]{1,0:T(8,128)(2,1)S(1)}, bf16[256,512]{1,0:T(8,128)(2,1)S(1)}, u32[]{:S(2)}, u32[]{:S(2)}) collective-permute-start(bf16[256,512]{1,0:T(8,128)(2,1)S(1)} %collective-permute-done.10), channel_id=1, source_target_pairs={{0,2},{2,4},{4,6},{6,8},{8,10},{10,12},{12,14},{14,16},{16,18},{18... | collective-permute-start | bytes 786440 | tf_op jit(solution)/shard_map/ppermute | solution.py:61
  132.3 17.5 %copy-start.6 = (bf16[256,512]{1,0:T(8,128)(2,1)}, bf16[256,512]{1,0:T(8,128)(2,1)S(1)}, u32[]{:S(2)}) copy-start(bf16[256,512]{1,0:T(8,128)(2,1)S(1)} %collective-permute-done.11) | copy-start | bytes 786436
  132.3 8.6 %collective-permute-start.12 = (bf16[256,512]{1,0:T(8,128)(2,1)S(1)}, bf16[256,512]{1,0:T(8,128)(2,1)}, u32[]{:S(2)}, u32[]{:S(2)}) collective-permute-start(bf16[256,512]{1,0:T(8,128)(2,1)S(1)} %collective-permute-done.11), channel_id=1, source_target_pairs={{0,2},{2,4},{4,6},{6,8},{8,10},{10,12},{12,14},{14,16},{16,18},{18... | collective-permute-start | bytes 786440 | tf_op jit(solution)/shard_map/ppermute | solution.py:61
  140.9 8.8 %collective-permute-start.13 = (bf16[256,512]{1,0:T(8,128)(2,1)}, bf16[256,512]{1,0:T(8,128)(2,1)}, u32[]{:S(2)}, u32[]{:S(2)}) collective-permute-start(bf16[256,512]{1,0:T(8,128)(2,1)} %collective-permute-done.12), channel_id=1, source_target_pairs={{0,2},{2,4},{4,6},{6,8},{8,10},{10,12},{12,14},{14,16},{16,18},{18... | collective-permute-start | bytes 786440 | tf_op jit(solution)/shard_map/ppermute | solution.py:61
  149.7 8.8 %collective-permute-start.14 = (bf16[256,512]{1,0:T(8,128)(2,1)}, bf16[256,512]{1,0:T(8,128)(2,1)}, u32[]{:S(2)}, u32[]{:S(2)}) collective-permute-start(bf16[256,512]{1,0:T(8,128)(2,1)} %collective-permute-done.13), channel_id=1, source_target_pairs={{0,2},{2,4},{4,6},{6,8},{8,10},{10,12},{12,14},{14,16},{16,18},{18... | collective-permute-start | bytes 786440 | tf_op jit(solution)/shard_map/ppermute | solution.py:61
  153.9 13.6 %copy-start.7 = (bf16[256,512]{1,0:T(8,128)(2,1)S(1)}, bf16[256,512]{1,0:T(8,128)(2,1)}, u32[]{:S(2)}) copy-start(bf16[256,512]{1,0:T(8,128)(2,1)} %copy-done.6) | copy-start | bytes 786436
  153.9 13.6 %copy-start.5 = (bf16[256,512]{1,0:T(8,128)(2,1)S(1)}, bf16[256,512]{1,0:T(8,128)(2,1)}, u32[]{:S(2)}) copy-start(bf16[256,512]{1,0:T(8,128)(2,1)} %copy-done.4) | copy-start | bytes 786436
  153.9 13.7 %copy-start.3 = (bf16[256,512]{1,0:T(8,128)(2,1)S(1)}, bf16[256,512]{1,0:T(8,128)(2,1)}, u32[]{:S(2)}) copy-start(bf16[256,512]{1,0:T(8,128)(2,1)} %copy-done.2) | copy-start | bytes 786436
Sparse Core Ops, SparseCore 0:
  25.0 56.9 all-gather.2
